TPU v7x, 32 devices: a whole 2x2x4 slice. The times are simulated.
32 devices in a mesh: seq: 8 (over z, y), head: 4 (over x, core).
Axes of the slice: x: 2, y: 2, z: 4, core: 2. Of those that a mesh axis runs over, the one named last changes fastest.
Arguments:
- queries: bfloat16 [4096, 8192], P(('seq', 'head')), may hold values from -8 to 8
- keys: bfloat16 [4096, 1024], P(('seq', 'head')), may hold values from -8 to 8
- values: bfloat16 [4096, 1024], P(('seq', 'head')), may hold values from -6 to 6
- selected: int32 [32, 8], P('seq'), may hold values from 0 to 31, as said below
- counts: int32 [32], P('seq'), may hold values from 1 to 8
- block_slot: int32 [32], P('seq'), may hold values from 0 to 31, as said below
Outputs:
- attended: bfloat16 [4096, 8192], P(('seq', 'head'))
Inputs may be any that keep to these rules, and one draw needn't show every extreme that they name: A permutation of 0 to 31. Block b's rows of keys and values start at row 128 * block_slot[b]; its owner shard is block_slot[b] // 4. The 4 blocks of one sequence shard (blocks s * 4 onward) have distinct owner shards, and block_slot[b] % 4 == b % 4. `selected`: row q lists its live entries first: entry 0 is q itself, the other live entries are distinct blocks of earlier sequence shards; entries from counts[q] on are 0. Over the live entries of the 4 rows of one sequence shard, at most 2 distinct blocks have the same owner shard, and in every draw some shard reaches 2 from some owner.
All inputs are finite; a program needn't handle non-finite values.
Results may differ from a plain program's by a relative error of at most 0.0049.
Values may be sent and summed in bfloat16 or wider, within the bound.
A program may use at most 128 MiB of HBM per device.

v0:
```python
import functools
import math

import jax
import jax.numpy as jnp
from jax import lax
from jax.experimental import pallas as pl
from jax.experimental.pallas import tpu as pltpu
from jax.sharding import PartitionSpec as P

QUERY_HEADS = 64
KEY_VALUE_HEADS = 8
HEAD_SIZE = 128
BLOCK_ROWS = 128
MESH = pl.DeviceIdType.MESH


def kernel(ns, nh, groups, entries, q_ref, k_ref, v_ref, sel_ref, cnt_ref, own_slot_ref, out_ref,
           qbuf, obuf, kcat, vcat, diag, slot_ref, slots_v, slots_s,
           hs, hr, qs, qr, us, ur, ds_, dr, ys, yr, os_, or_, ss, sr, slot_sem, *kv):
    s = lax.axis_index("seq")
    h = lax.axis_index("head")
    ysz = 2 if ns % 2 == 0 else 1
    zsz = ns // ysz
    z = s // ysz
    y = s % ysz
    y_peer = s + 1 - 2 * y
    width = qbuf.shape[3]
    heads_per_group = width // HEAD_SIZE
    rotation = [nh // 2] + [d for d in range(nh - 1, 0, -1) if d != nh // 2]

    def remote(src, dst, send, recv, dev):
        return pltpu.make_async_remote_copy(
            src_ref=src, dst_ref=dst, send_sem=send, recv_sem=recv,
            device_id=dev, device_id_type=MESH)

    lane = lax.broadcasted_iota(jnp.int32, (1, 128), 1)
    slot_row = jnp.zeros((1, 128), jnp.int32)
    for i in range(sel_ref.shape[0]):
        slot_row = jnp.where(lane == i, own_slot_ref[i], slot_row)
    slot_ref[...] = slot_row

    barrier = pltpu.get_barrier_semaphore()
    for d in range(1, nh):
        pl.semaphore_signal(barrier, inc=1, device_id=(s, (h + d) % nh), device_id_type=MESH)
    for d in range(1, ns):
        pl.semaphore_signal(barrier, inc=1, device_id=((s + d) % ns, h), device_id_type=MESH)
    pl.semaphore_wait(barrier, nh - 1 + ns - 1)

    def lanes(unit, size):
        return pl.ds(pl.multiple_of(unit * size, size), size)

    def kv_head(g, t, d):
        peer = (h + d) % nh
        src = (k_ref, v_ref)[t]
        return remote(src.at[:, lanes(peer * groups + g, HEAD_SIZE)], kv[g].at[s * nh + h, t],
                      hs.at[g, t, d - 1], hr.at[g, t, d - 1], (s, peer))

    def kv_head_in(g, t, d):
        peer = (h + nh - d) % nh
        src = (k_ref, v_ref)[t]
        return remote(src.at[:, lanes(peer * groups + g, HEAD_SIZE)], kv[g].at[s * nh + peer, t],
                      hs.at[g, t, d - 1], hr.at[g, t, d - 1], (s, peer))

    def q_head(g, d):
        peer = (h + d) % nh
        return remote(q_ref.at[:, lanes(peer * groups + g, width)], qbuf.at[g, h],
                      qs.at[g, d - 1], qr.at[g, d - 1], (s, peer))

    def q_head_in(g, d):
        peer = (h + nh - d) % nh
        return remote(q_ref.at[:, lanes(peer * groups + g, width)], qbuf.at[g, peer],
                      qs.at[g, d - 1], qr.at[g, d - 1], (s, peer))

    def slot_out(d):
        return remote(slot_ref, slots_v.at[s], ss.at[d - 1], sr.at[d - 1], ((s + d) % ns, h))

    def slot_in(d):
        peer = (s + ns - d) % ns
        return remote(slot_ref, slots_v.at[peer], ss.at[d - 1], sr.at[d - 1], (peer, h))

    for g in range(groups):
        for d in rotation:
            for t in range(2):
                kv_head(g, t, d).start()
    for d in range(1, ns):
        slot_out(d).start()
    for g in range(groups):
        for d in rotation:
            q_head(g, d).start()

    for g in range(groups):
        kv[g][s * nh + h, 0] = k_ref[:, lanes(h * groups + g, HEAD_SIZE)]
        kv[g][s * nh + h, 1] = v_ref[:, lanes(h * groups + g, HEAD_SIZE)]
        qbuf[g, h] = q_ref[:, lanes(h * groups + g, width)]
    slots_v[s] = slot_ref[...]
    pair_rows = 2 * BLOCK_ROWS
    row = lax.rem(lax.broadcasted_iota(jnp.int32, (pair_rows, BLOCK_ROWS), 0), BLOCK_ROWS)
    col = lax.broadcasted_iota(jnp.int32, (pair_rows, BLOCK_ROWS), 1)
    diag[...] = jnp.where(col <= row, 0.0, -jnp.inf).astype(jnp.float32)
    vcat[:, HEAD_SIZE:] = jnp.ones((entries * BLOCK_ROWS, HEAD_SIZE), jnp.bfloat16)

    half = nh // 2

    def early(g):
        return ysz > 1 and nh > 2 and g == groups - 1

    def part(g, shard, piece):
        lo, size = ((0, half), (half, nh - half), (nh - 1, 1))[piece]
        return kv[g].at[pl.ds(shard * nh + lo, size)]

    def cross_part(g, shard, piece):
        if piece == 1 and early(g):
            return kv[g].at[pl.ds(shard * nh + half, nh - 1 - half)]
        return part(g, shard, piece)

    def up(g, p, t, shard, dev):
        ref = part(g, shard, p)
        return remote(ref, ref, us.at[g, p, t], ur.at[g, p, t], (dev, h))

    def down(g, p, t, shard, dev):
        ref = part(g, shard, p)
        return remote(ref, ref, ds_.at[g, p, t], dr.at[g, p, t], (dev, h))

    def across(g, p, i, shard):
        ref = cross_part(g, shard, p)
        return remote(ref, ref, ys.at[g, p, i], yr.at[g, p, i], (y_peer, h))

    def pieces(g):
        return (0, 1, 2) if early(g) else (0, 1)

    def column(p):
        return y_peer if p == 2 else s

    def send_both(g, p):
        if zsz > 1:
            @pl.when(z < zsz - 1)
            def _():
                up(g, p, 0, column(p), s + ysz).start()

            @pl.when(z > 0)
            def _():
                down(g, p, 0, column(p), s - ysz).start()

    def gather_z(g):
        for d in rotation:
            for t in range(2):
                kv_head_in(g, t, d).wait_recv()
        if early(g):
            across(g, 2, 0, s).start()
        send_both(g, 0)
        send_both(g, 1)

    def gather_y(g):
        if ysz > 1:
            across(g, 0, 0, s).start()
            across(g, 1, 0, s).start()
        if early(g):
            across(g, 2, 0, y_peer).wait_recv()
            send_both(g, 2)

    def gather_step(g, t):
        for p in pieces(g):
            below = column(p) - (1 + t) * ysz
            above = column(p) + (1 + t) * ysz

            @pl.when(z - 1 - t >= 0)
            def _():
                up(g, p, t, below, s).wait_recv()
                if t + 1 < zsz - 1:
                    @pl.when(z < zsz - 1)
                    def _():
                        up(g, p, t + 1, below, s + ysz).start()
                if ysz > 1 and p < 2:
                    across(g, p, 1 + t, below).start()

            @pl.when(z + 1 + t <= zsz - 1)
            def _():
                down(g, p, t, above, s).wait_recv()
                if t + 1 < zsz - 1:
                    @pl.when(z > 0)
                    def _():
                        down(g, p, t + 1, above, s - ysz).start()
                if ysz > 1 and p < 2:
                    across(g, p, zsz + t, above).start()

    def gather_end(g):
        if ysz > 1:
            for p in range(2):
                across(g, p, 0, y_peer).wait_recv()
            for t in range(zsz - 1):
                for p in range(2):
                    @pl.when(z - 1 - t >= 0)
                    def _():
                        across(g, p, 1 + t, y_peer - (1 + t) * ysz).wait_recv()

                    @pl.when(z + 1 + t <= zsz - 1)
                    def _():
                        across(g, p, zsz + t, y_peer + (1 + t) * ysz).wait_recv()

    def gather_drain(g):
        for p in pieces(g):
            if ysz > 1:
                across(g, p, 0, s).wait_send()
            for t in range(zsz - 1):
                @pl.when((z < zsz - 1) & (z - t >= 0))
                def _():
                    up(g, p, t, column(p) - t * ysz, s + ysz).wait_send()

                @pl.when((z > 0) & (z + t <= zsz - 1))
                def _():
                    down(g, p, t, column(p) + t * ysz, s - ysz).wait_send()
                if ysz > 1 and p < 2:
                    @pl.when(z - 1 - t >= 0)
                    def _():
                        across(g, p, 1 + t, s - (1 + t) * ysz).wait_send()

                    @pl.when(z + 1 + t <= zsz - 1)
                    def _():
                        across(g, p, zsz + t, s + (1 + t) * ysz).wait_send()

    factor = math.log2(math.e) / math.sqrt(HEAD_SIZE)
    blk_seq = sel_ref.shape[0]

    def fetch(g, j):
        for e in range(entries):
            b = sel_ref[j, e]
            place = slots_s[lax.div(b, blk_seq), 0, lax.rem(b, blk_seq)]
            rows = slice(e * BLOCK_ROWS, (e + 1) * BLOCK_ROWS)
            kcat[rows, :] = kv[g][place, 0]
            vcat[rows, :HEAD_SIZE] = kv[g][place, 1]

    def attend(g, j):
        rest = lax.broadcasted_iota(jnp.int32, (1, (entries - 1) * BLOCK_ROWS), 1) + BLOCK_ROWS
        bias = jnp.where(rest < cnt_ref[j] * BLOCK_ROWS, 0.0, -jnp.inf).astype(jnp.float32)

        def pair(i, _):
            cols = pl.multiple_of(i * 2 * HEAD_SIZE, 2 * HEAD_SIZE)
            q2 = qbuf[g, j, :, pl.ds(cols, 2 * HEAD_SIZE)]
            q2 = jnp.concatenate([q2[:, :HEAD_SIZE], q2[:, HEAD_SIZE:]], axis=0)
            scores = lax.dot_general(q2, kcat[...], (((1,), (1,)), ((), ())),
                                     preferred_element_type=jnp.float32)
            own = scores[:, :BLOCK_ROWS] + diag[...]
            others = scores[:, BLOCK_ROWS:] + bias
            scores = jnp.concatenate([own, others], axis=1)
            top = jnp.max(scores, axis=1, keepdims=True)
            weights = jnp.exp2((scores - top) * factor).astype(jnp.bfloat16)
            mixed = jnp.dot(weights, vcat[...], preferred_element_type=jnp.float32)
            result = (mixed[:, :HEAD_SIZE] / mixed[:, HEAD_SIZE:]).astype(jnp.bfloat16)
            obuf[g, j, :, pl.ds(cols, HEAD_SIZE)] = result[:BLOCK_ROWS]
            obuf[g, j, :, pl.ds(cols + HEAD_SIZE, HEAD_SIZE)] = result[BLOCK_ROWS:]
            return 0

        lax.fori_loop(0, heads_per_group // 2, pair, 0, unroll=True)

    def result_out(g, d):
        peer = (h + d) % nh
        return remote(obuf.at[g, peer], out_ref.at[:, lanes(h * groups + g, width)],
                      os_.at[g, d - 1], or_.at[g, d - 1], (s, peer))

    def result_in(g, d):
        peer = (h + nh - d) % nh
        return remote(obuf.at[g, peer], out_ref.at[:, lanes(peer * groups + g, width)],
                      os_.at[g, d - 1], or_.at[g, d - 1], (s, peer))

    def slot_table():
        for d in range(1, ns):
            slot_in(d).wait_recv()
        slot_copy = pltpu.make_async_copy(slots_v, slots_s, slot_sem)
        slot_copy.start()
        slot_copy.wait()

    if nh == 4:
        order = [2, 3 - 2 * (h % 2), 1 + 2 * (h % 2), 0]
    else:
        order = rotation + [0]
    gather_z(0)
    gather_y(0)
    for t in range(zsz - 2):
        gather_step(0, t)
    pending = None
    for g in range(groups):
        more = g + 1 < groups
        if more:
            gather_z(g + 1)
        if g == 0 and zsz > 1:
            gather_step(0, zsz - 2)
        steps = []
        if more:
            gather_y(g + 1)
            steps = list(range(zsz - 1))
            if steps:
                gather_step(g + 1, steps.pop(0))
        if g == 0:
            slot_table()
        gather_end(g)
        for n, d in enumerate(order):
            own = n == len(order) - 1
            j = (h + d) % nh
            fetch(g, j)
            if pending is not None:
                result_out(*pending).start()
                pending = None
            if not own:
                q_head_in(g, nh - d).wait_recv()
            if n >= len(order) // 2 and len(steps) > 1:
                gather_step(g + 1, steps.pop(0))
            attend(g, j)
            if own:
                out_ref[:, lanes(h * groups + g, width)] = obuf[g, h]
            else:
                pending = (g, d)
        for t in steps:
            gather_step(g + 1, t)

    for g in range(groups):
        gather_drain(g)
        for d in rotation:
            for t in range(2):
                kv_head(g, t, d).wait_send()
            q_head(g, d).wait_send()
    for d in range(1, ns):
        slot_out(d).wait_send()
    for g in range(groups):
        for d in rotation:
            result_out(g, d).wait_send()
            result_in(g, d).wait_recv()


def body(queries, keys, values, selected, counts, block_slot):
    ns = lax.axis_size("seq")
    nh = lax.axis_size("head")
    blk_seq, entries = selected.shape
    rows = queries.shape[0]
    groups = keys.shape[1] // HEAD_SIZE // nh
    width = queries.shape[1] // nh // groups
    assert rows == BLOCK_ROWS and blk_seq == nh
    vmem = pl.BlockSpec(memory_space=pltpu.VMEM)
    smem = pl.BlockSpec(memory_space=pltpu.SMEM)
    zsz = ns // (2 if ns % 2 == 0 else 1)
    dma = pltpu.SemaphoreType.DMA
    steps = max(zsz - 1, 1)
    return pl.pallas_call(
        functools.partial(kernel, ns, nh, groups, entries),
        out_shape=jax.ShapeDtypeStruct(queries.shape, jnp.bfloat16),
        in_specs=[vmem, vmem, vmem, smem, smem, smem],
        out_specs=vmem,
        scratch_shapes=[
            pltpu.VMEM((groups, nh, rows, width), jnp.bfloat16),
            pltpu.VMEM((groups, nh, rows, width), jnp.bfloat16),
            pltpu.VMEM((entries * BLOCK_ROWS, HEAD_SIZE), jnp.bfloat16),
            pltpu.VMEM((entries * BLOCK_ROWS, 2 * HEAD_SIZE), jnp.bfloat16),
            pltpu.VMEM((2 * BLOCK_ROWS, BLOCK_ROWS), jnp.float32),
            pltpu.VMEM((1, 128), jnp.int32),
            pltpu.VMEM((ns, 1, 128), jnp.int32),
            pltpu.SMEM((ns, 1, 128), jnp.int32),
            dma((groups, 2, nh - 1)), dma((groups, 2, nh - 1)),
            dma((groups, nh - 1)), dma((groups, nh - 1)),
            dma((groups, 3, steps)), dma((groups, 3, steps)),
            dma((groups, 3, steps)), dma((groups, 3, steps)),
            dma((groups, 3, 2 * zsz)), dma((groups, 3, 2 * zsz)),
            dma((groups, nh - 1)), dma((groups, nh - 1)),
            dma((ns - 1,)), dma((ns - 1,)),
            dma,
        ] + [pltpu.VMEM((ns * nh, 2, BLOCK_ROWS, HEAD_SIZE), jnp.bfloat16)] * groups,
        compiler_params=pltpu.CompilerParams(
            collective_id=0, has_side_effects=True, vmem_limit_bytes=60 * 1024 * 1024),
        name="block_attention",
    )(queries, keys, values, selected, counts, block_slot)


def solution(mesh):
    return jax.shard_map(
        body,
        mesh=mesh,
        in_specs=(
            P(("seq", "head"), None),
            P(("seq", "head"), None),
            P(("seq", "head"), None),
            P("seq", None),
            P("seq"),
            P("seq"),
        ),
        out_specs=P(("seq", "head"), None),
        check_vma=False,
    )
```

profile of v0, /device:TPU:0, one launch (start us, length us, event | category | flops | bytes accessed | tf_op | source)
XLA Modules:
  0.0 78.9 jit_solution(7053085162907909545)
XLA Ops:
  0.0 75.8 %block_attention.1 = bf16[128,8192]{1,0:T(8,128)(2,1)} custom-call(bf16[128,8192]{1,0:T(8,128)(2,1)} %q_ref.1, bf16[128,1024]{1,0:T(8,128)(2,1)} %k_ref.1, bf16[128,1024]{1,0:T(8,128)(2,1)} %v_ref.1, s32[4,8]{1,0:T(4,128)} %sel_ref.1, s32[4]{0:T(128)} %cnt_ref.1, s32[4]{0:T(128)} %own_slot_ref.1), custom_call_target="tpu_custom_call" | custom-call | tf_op jit(solution)/shard_map/block_attention/pallas_call | solution.py:343
  75.8 3.1 %copy.8 = bf16[128,8192]{1,0:T(8,128)(2,1)} copy(bf16[128,8192]{1,0:T(8,128)(2,1)} %block_attention.1) | data formatting | bytes 4194304
where the time goes:
time: 79.1 us; the launch traced here: 78.9 us
  Pallas kernels  75.8 us (96%)
  local copies, waits for them, and re-layouts  3.1 us (4%)
    pallas_call x1, Pallas kernels, body(): pl.pallas_call(functools.partial(kernel, ns, nh, groups, entries), out_sh...  75.8 us
    unnamed x1, local copies, waits for them, and re-layouts  3.1 us

commit v1 on v0

v1 whole, which is shorter than its diff:
```python
import functools
import math

import jax
import jax.numpy as jnp
from jax import lax
from jax.experimental import pallas as pl
from jax.experimental.pallas import tpu as pltpu
from jax.sharding import PartitionSpec as P

QUERY_HEADS = 64
KEY_VALUE_HEADS = 8
HEAD_SIZE = 128
BLOCK_ROWS = 128
Y_SIZE = 2
PER_OWNER = 2
MESH = pl.DeviceIdType.MESH


def kernel(ns, nh, groups, entries, q_ref, k_ref, v_ref, sel_ref, cnt_ref, own_slot_ref, out_ref,
           qbuf, obuf, kcat, vcat, diag, stage, row_ref, rows_v, rows_s, plan_v, plan_s,
           hs, hr, qs, qr, us, ur, ds_, dr, ys, yr, os_, or_, ss, sr, local_sem, *kv):
    s = lax.axis_index("seq")
    h = lax.axis_index("head")
    ysz = Y_SIZE
    zsz = ns // ysz
    z = s // ysz
    y = s % ysz
    y_peer = s + 1 - 2 * y
    half = nh // 2
    side = h // half
    spot = h % half
    width = qbuf.shape[3]
    heads_per_group = width // HEAD_SIZE
    blk_seq = sel_ref.shape[0]
    near = [(0, i) for i in range(1, half)]
    far = [(1, i) for i in range(half)]
    ways = near + far

    def remote(src, dst, send, recv, dev):
        return pltpu.make_async_remote_copy(
            src_ref=src, dst_ref=dst, send_sem=send, recv_sem=recv,
            device_id=dev, device_id_type=MESH)

    def target(w):
        flip, i = ways[w]
        return (side + flip) % 2 * half + (spot + i) % half

    def origin(w):
        flip, i = ways[w]
        return (side + flip) % 2 * half + (spot + half - i) % half

    lane = lax.broadcasted_iota(jnp.int32, (1, 128), 1)
    info = jnp.zeros((1, 128), jnp.int32)
    for j in range(blk_seq):
        info = jnp.where(lane == j, own_slot_ref[j], info)
        for e in range(entries):
            block = jnp.where(e < cnt_ref[j], sel_ref[j, e], sel_ref[j, 0])
            info = jnp.where(lane == blk_seq + j * entries + e, block, info)
    row_ref[...] = info

    barrier = pltpu.get_barrier_semaphore()
    for d in range(1, nh):
        pl.semaphore_signal(barrier, inc=1, device_id=(s, (h + d) % nh), device_id_type=MESH)
    for d in range(1, ns):
        pl.semaphore_signal(barrier, inc=1, device_id=((s + d) % ns, h), device_id_type=MESH)
    pl.semaphore_wait(barrier, nh - 1 + ns - 1)

    def lanes(unit, size):
        return pl.ds(pl.multiple_of(unit * size, size), size)

    def kv_head(g, t, w, peer, place):
        src = (k_ref, v_ref)[t]
        return remote(src.at[:, lanes(peer * groups + g, HEAD_SIZE)], kv[g].at[z * nh + place, t],
                      hs.at[g, t, w], hr.at[g, t, w], (s, peer))

    def kv_head_out(g, t, w):
        return kv_head(g, t, w, target(w), h)

    def kv_head_in(g, t, w):
        return kv_head(g, t, w, origin(w), origin(w))

    def q_head(g, w, peer, place):
        return remote(q_ref.at[:, lanes(peer * groups + g, width)], qbuf.at[g, place],
                      qs.at[g, w], qr.at[g, w], (s, peer))

    def q_head_out(g, w):
        return q_head(g, w, target(w), h)

    def q_head_in(g, w):
        return q_head(g, w, origin(w), origin(w))

    def row_out(d):
        return remote(row_ref, rows_v.at[s], ss.at[d - 1], sr.at[d - 1], ((s + d) % ns, h))

    def row_in(d):
        peer = (s + ns - d) % ns
        return remote(row_ref, rows_v.at[peer], ss.at[d - 1], sr.at[d - 1], (peer, h))

    for g in range(groups):
        for w in range(len(ways)):
            for t in range(2):
                kv_head_out(g, t, w).start()
        if g == 0:
            for d in range(1, ns):
                row_out(d).start()
    for g in range(groups):
        for w in reversed(range(len(ways))):
            q_head_out(g, w).start()

    for g in range(groups):
        kv[g][z * nh + h, 0] = k_ref[:, lanes(h * groups + g, HEAD_SIZE)]
        kv[g][z * nh + h, 1] = v_ref[:, lanes(h * groups + g, HEAD_SIZE)]
        qbuf[g, h] = q_ref[:, lanes(h * groups + g, width)]
    rows_v[s] = row_ref[...]
    pair_rows = 2 * BLOCK_ROWS
    row = lax.rem(lax.broadcasted_iota(jnp.int32, (pair_rows, BLOCK_ROWS), 0), BLOCK_ROWS)
    col = lax.broadcasted_iota(jnp.int32, (pair_rows, BLOCK_ROWS), 1)
    diag[...] = jnp.where(col <= row, 0.0, -jnp.inf).astype(jnp.float32)
    vcat[:, HEAD_SIZE:] = jnp.ones((entries * BLOCK_ROWS, HEAD_SIZE), jnp.bfloat16)

    def part(g, zz, p):
        lo = (side + p) % 2 * half
        return kv[g].at[pl.ds(zz * nh + lo, half)]

    def up(g, p, t, zz, dev):
        ref = part(g, zz, p)
        return remote(ref, ref, us.at[g, p, t], ur.at[g, p, t], (dev, h))

    def down(g, p, t, zz, dev):
        ref = part(g, zz, p)
        return remote(ref, ref, ds_.at[g, p, t], dr.at[g, p, t], (dev, h))

    def across(g, r, zz):
        return remote(stage.at[g, pl.ds(zz * PER_OWNER, PER_OWNER)],
                      kv[g].at[pl.ds(zsz * nh + zz * PER_OWNER, PER_OWNER)],
                      ys.at[g, r], yr.at[g, r], (y_peer, h))

    def send_across(g, r, zz):
        for k in range(PER_OWNER):
            pick = plan_s[1 + k, r]
            for t in range(2):
                chosen = kv[g][zz * nh + nh - 1, t]
                for j in reversed(range(nh - 1)):
                    chosen = jnp.where(pick == j, kv[g][zz * nh + j, t], chosen)
                stage[g, zz * PER_OWNER + k, t] = chosen
        across(g, r, zz).start()

    def send_both(g, p):
        if zsz > 1:
            @pl.when(z < zsz - 1)
            def _():
                up(g, p, 0, z, s + ysz).start()

            @pl.when(z > 0)
            def _():
                down(g, p, 0, z, s - ysz).start()

    def gather_z(g):
        for w in range(len(ways)):
            if w == len(near):
                send_both(g, 0)
            for t in range(2):
                kv_head_in(g, t, w).wait_recv()
        send_both(g, 1)

    def gather_step(g, t):
        @pl.when(z - 1 - t >= 0)
        def _():
            below = z - 1 - t
            for p in range(2):
                up(g, p, t, below, s).wait_recv()
                if t + 1 < zsz - 1:
                    @pl.when(z < zsz - 1)
                    def _():
                        up(g, p, t + 1, below, s + ysz).start()
            send_across(g, 1 + t, below)

        @pl.when(z + 1 + t <= zsz - 1)
        def _():
            above = z + 1 + t
            for p in range(2):
                down(g, p, t, above, s).wait_recv()
                if t + 1 < zsz - 1:
                    @pl.when(z > 0)
                    def _():
                        down(g, p, t + 1, above, s - ysz).start()
            send_across(g, zsz + t, above)

    def each_owner(call):
        call(0, z)
        for t in range(zsz - 1):
            @pl.when(z - 1 - t >= 0)
            def _():
                call(1 + t, z - 1 - t)

            @pl.when(z + 1 + t <= zsz - 1)
            def _():
                call(zsz + t, z + 1 + t)

    def gather_end(g):
        each_owner(lambda r, zz: across(g, r, zz).wait_recv())

    def gather_drain(g):
        each_owner(lambda r, zz: across(g, r, zz).wait_send())
        for p in range(2):
            for t in range(zsz - 1):
                @pl.when((z < zsz - 1) & (z - t >= 0))
                def _():
                    up(g, p, t, z - t, s + ysz).wait_send()

                @pl.when((z > 0) & (z + t <= zsz - 1))
                def _():
                    down(g, p, t, z + t, s - ysz).wait_send()

    def plan():
        for d in range(1, ns):
            row_in(d).wait_recv()
        table = pltpu.make_async_copy(rows_v, rows_s, local_sem)
        table.start()
        table.wait()

        def slot_of(shard, i):
            b = rows_s[shard, 0, blk_seq + i]
            slot = rows_s[lax.div(b, blk_seq), 0, lax.rem(b, blk_seq)]
            owner = lax.div(slot, nh)
            return lax.rem(slot, nh), lax.div(owner, ysz), lax.rem(owner, ysz)

        first = jnp.full((1, 128), nh, jnp.int32)
        last = jnp.full((1, 128), -1, jnp.int32)
        for i in range(blk_seq * entries):
            j, oz, oy = slot_of(y_peer, i)
            r = jnp.where(oz < z, z - oz, jnp.where(oz > z, zsz - 1 + oz - z, 0))
            hit = lane == jnp.where(oy == y, r, -1)
            first = jnp.where(hit, jnp.minimum(first, j), first)
            last = jnp.where(hit, jnp.maximum(last, j), last)
        mine = [slot_of(s, i) for i in range(blk_seq * entries)]
        js = jnp.zeros((1, 128), jnp.int32)
        ozs = jnp.zeros((1, 128), jnp.int32)
        oys = jnp.zeros((1, 128), jnp.int32)
        for i, (j, oz, oy) in enumerate(mine):
            js = jnp.where(lane == i, j, js)
            ozs = jnp.where(lane == i, oz, ozs)
            oys = jnp.where(lane == i, oy, oys)
        second = jnp.zeros((1, 128), jnp.int32)
        for j, oz, oy in mine:
            second = jnp.where((ozs == oz) & (oys == oy) & (js > j), 1, second)
        place = jnp.where(oys == y, ozs * nh + js, zsz * nh + ozs * PER_OWNER + second)
        plan_v[0:1, :] = place
        plan_v[1:2, :] = first
        plan_v[2:3, :] = last
        copy = pltpu.make_async_copy(plan_v, plan_s, local_sem)
        copy.start()
        copy.wait()

    factor = math.log2(math.e) / math.sqrt(HEAD_SIZE)

    def fetch(g, j):
        for e in range(entries):
            place = plan_s[0, j * entries + e]
            rows = slice(e * BLOCK_ROWS, (e + 1) * BLOCK_ROWS)
            kcat[rows, :] = kv[g][place, 0]
            vcat[rows, :HEAD_SIZE] = kv[g][place, 1]

    def attend(g, j):
        rest = lax.broadcasted_iota(jnp.int32, (1, (entries - 1) * BLOCK_ROWS), 1) + BLOCK_ROWS
        bias = jnp.where(rest < cnt_ref[j] * BLOCK_ROWS, 0.0, -jnp.inf).astype(jnp.float32)

        def pair(i, _):
            cols = pl.multiple_of(i * 2 * HEAD_SIZE, 2 * HEAD_SIZE)
            q2 = qbuf[g, j, :, pl.ds(cols, 2 * HEAD_SIZE)]
            q2 = jnp.concatenate([q2[:, :HEAD_SIZE], q2[:, HEAD_SIZE:]], axis=0)
            scores = lax.dot_general(q2, kcat[...], (((1,), (1,)), ((), ())),
                                     preferred_element_type=jnp.float32)
            own = scores[:, :BLOCK_ROWS] + diag[...]
            others = scores[:, BLOCK_ROWS:] + bias
            scores = jnp.concatenate([own, others], axis=1)
            top = jnp.max(scores, axis=1, keepdims=True)
            weights = jnp.exp2((scores - top) * factor).astype(jnp.bfloat16)
            mixed = jnp.dot(weights, vcat[...], preferred_element_type=jnp.float32)
            result = (mixed[:, :HEAD_SIZE] / mixed[:, HEAD_SIZE:]).astype(jnp.bfloat16)
            obuf[g, j, :, pl.ds(cols, HEAD_SIZE)] = result[:BLOCK_ROWS]
            obuf[g, j, :, pl.ds(cols + HEAD_SIZE, HEAD_SIZE)] = result[BLOCK_ROWS:]
            return 0

        lax.fori_loop(0, heads_per_group // 2, pair, 0, unroll=True)

    def result(g, w, peer, mine):
        return remote(obuf.at[g, peer], out_ref.at[:, lanes(mine * groups + g, width)],
                      os_.at[g, w], or_.at[g, w], (s, peer))

    def result_out(g, w):
        return result(g, w, target(w), h)

    def result_in(g, w):
        return result(g, w, origin(w), origin(w))

    def back(w):
        flip, i = ways[w]
        return ways.index((flip, (half - i) % half))

    order = list(range(len(near), len(ways))) + list(range(len(near))) + [None]
    gather_z(0)
    plan()
    send_across(0, 0, z)
    for t in range(zsz - 2):
        gather_step(0, t)
    pending = None
    for g in range(groups):
        more = g + 1 < groups
        if more:
            gather_z(g + 1)
        if g == 0 and zsz > 1:
            gather_step(0, zsz - 2)
        steps = []
        if more:
            send_across(g + 1, 0, z)
            steps = list(range(zsz - 1))
            if steps:
                gather_step(g + 1, steps.pop(0))
        gather_end(g)
        for n, w in enumerate(order):
            own = w is None
            j = h if own else target(w)
            fetch(g, j)
            if pending is not None:
                result_out(*pending).start()
                pending = None
            if not own:
                q_head_in(g, back(w)).wait_recv()
            if n >= len(order) // 2 and len(steps) > 1:
                gather_step(g + 1, steps.pop(0))
            attend(g, j)
            if own:
                out_ref[:, lanes(h * groups + g, width)] = obuf[g, h]
            else:
                pending = (g, w)
        for t in steps:
            gather_step(g + 1, t)

    for g in range(groups):
        gather_drain(g)
        for w in range(len(ways)):
            for t in range(2):
                kv_head_out(g, t, w).wait_send()
            q_head_out(g, w).wait_send()
    for d in range(1, ns):
        row_out(d).wait_send()
    for g in range(groups):
        for w in range(len(ways)):
            result_out(g, w).wait_send()
            result_in(g, w).wait_recv()


def body(queries, keys, values, selected, counts, block_slot):
    ns = lax.axis_size("seq")
    nh = lax.axis_size("head")
    blk_seq, entries = selected.shape
    rows = queries.shape[0]
    groups = keys.shape[1] // HEAD_SIZE // nh
    width = queries.shape[1] // nh // groups
    assert rows == BLOCK_ROWS and blk_seq == nh and nh % 2 == 0 and ns % Y_SIZE == 0
    vmem = pl.BlockSpec(memory_space=pltpu.VMEM)
    smem = pl.BlockSpec(memory_space=pltpu.SMEM)
    zsz = ns // Y_SIZE
    dma = pltpu.SemaphoreType.DMA
    steps = max(zsz - 1, 1)
    held = zsz * (nh + PER_OWNER)
    return pl.pallas_call(
        functools.partial(kernel, ns, nh, groups, entries),
        out_shape=jax.ShapeDtypeStruct(queries.shape, jnp.bfloat16),
        in_specs=[vmem, vmem, vmem, smem, smem, smem],
        out_specs=vmem,
        scratch_shapes=[
            pltpu.VMEM((groups, nh, rows, width), jnp.bfloat16),
            pltpu.VMEM((groups, nh, rows, width), jnp.bfloat16),
            pltpu.VMEM((entries * BLOCK_ROWS, HEAD_SIZE), jnp.bfloat16),
            pltpu.VMEM((entries * BLOCK_ROWS, 2 * HEAD_SIZE), jnp.bfloat16),
            pltpu.VMEM((2 * BLOCK_ROWS, BLOCK_ROWS), jnp.float32),
            pltpu.VMEM((groups, zsz * PER_OWNER, 2, BLOCK_ROWS, HEAD_SIZE), jnp.bfloat16),
            pltpu.VMEM((1, 128), jnp.int32),
            pltpu.VMEM((ns, 1, 128), jnp.int32),
            pltpu.SMEM((ns, 1, 128), jnp.int32),
            pltpu.VMEM((8, 128), jnp.int32),
            pltpu.SMEM((8, 128), jnp.int32),
            dma((groups, 2, nh - 1)), dma((groups, 2, nh - 1)),
            dma((groups, nh - 1)), dma((groups, nh - 1)),
            dma((groups, 2, steps)), dma((groups, 2, steps)),
            dma((groups, 2, steps)), dma((groups, 2, steps)),
            dma((groups, 2 * zsz)), dma((groups, 2 * zsz)),
            dma((groups, nh - 1)), dma((groups, nh - 1)),
            dma((ns - 1,)), dma((ns - 1,)),
            dma,
        ] + [pltpu.VMEM((held, 2, BLOCK_ROWS, HEAD_SIZE), jnp.bfloat16)] * groups,
        compiler_params=pltpu.CompilerParams(
            collective_id=0, has_side_effects=True, vmem_limit_bytes=60 * 1024 * 1024),
        name="block_attention",
    )(queries, keys, values, selected, counts, block_slot)


def solution(mesh):
    return jax.shard_map(
        body,
        mesh=mesh,
        in_specs=(
            P(("seq", "head"), None),
            P(("seq", "head"), None),
            P(("seq", "head"), None),
            P("seq", None),
            P("seq"),
            P("seq"),
        ),
        out_specs=P(("seq", "head"), None),
        check_vma=False,
    )
```

time: 79.1 us -> 71.4 us (0.903)
  Pallas kernels: 75.8 us -> 67.9 us
    pallas_call x1, Pallas kernels: 75.8 us -> 67.9 us  [body(): pl.pallas_call(functools.partial(kernel, ns, nh, groups, entries), out_sh...]
where the time goes in v1:
time: 71.4 us; the launch traced here: 71 us
  Pallas kernels  67.9 us (95%)
  local copies, waits for them, and re-layouts  3.1 us (4%)
    pallas_call x1, Pallas kernels, body(): pl.pallas_call(functools.partial(kernel, ns, nh, groups, entries), out_sh...  67.9 us
    unnamed x1, local copies, waits for them, and re-layouts  3.1 us

profile of v1, /device:TPU:0, one launch (start us, length us, event | category | flops | bytes accessed | tf_op | source)
XLA Modules:
  0.0 71.0 jit_solution(10474389395957736465)
XLA Ops:
  0.0 67.9 %block_attention.1 = bf16[128,8192]{1,0:T(8,128)(2,1)} custom-call(bf16[128,8192]{1,0:T(8,128)(2,1)} %q_ref.1, bf16[128,1024]{1,0:T(8,128)(2,1)} %k_ref.1, bf16[128,1024]{1,0:T(8,128)(2,1)} %v_ref.1, s32[4,8]{1,0:T(4,128)} %sel_ref.1, s32[4]{0:T(128)} %cnt_ref.1, s32[4]{0:T(128)} %own_slot_ref.1), custom_call_target="tpu_custom_call" | custom-call | tf_op jit(solution)/shard_map/block_attention/pallas_call | solution.py:369
  67.9 3.1 %copy.8 = bf16[128,8192]{1,0:T(8,128)(2,1)} copy(bf16[128,8192]{1,0:T(8,128)(2,1)} %block_attention.1) | data formatting | bytes 4194304

commit v2 on v1

v2 whole, which is shorter than its diff:
```python
import functools
import math

import jax
import jax.numpy as jnp
from jax import lax
from jax.experimental import pallas as pl
from jax.experimental.pallas import tpu as pltpu
from jax.sharding import PartitionSpec as P

QUERY_HEADS = 64
KEY_VALUE_HEADS = 8
HEAD_SIZE = 128
BLOCK_ROWS = 128
Y_SIZE = 2
PER_OWNER = 2
MESH = pl.DeviceIdType.MESH


def kernel(ns, nh, heads, entries, q_hbm, k_hbm, v_hbm, sel_ref, cnt_ref, own_slot_ref, out_ref,
           qv, kvin, qbuf, obuf, kcat, vcat, diag, stage, rows_v, rows_s, plan_v, plan_s, place_v, place_s,
           ins, local_sem, hs, hr, qs, qr, us, ur, ds_, dr, ys, yr, cs, cr, os_, or_, ss, sr, *kv):
    s = lax.axis_index("seq")
    h = lax.axis_index("head")
    ysz = Y_SIZE
    zsz = ns // ysz
    hops = max(zsz - 1, 1)
    z = s // ysz
    y = s % ysz
    y_peer = s + 1 - 2 * y
    half = nh // 2
    side = h // half
    c = h % half
    partner = side * half + 1 - c
    x_peer = (1 - side) * half + c
    width = qbuf.shape[2]
    pairs = width // (2 * HEAD_SIZE)
    blk_seq = sel_ref.shape[0]

    def remote(src, dst, send, recv, dev):
        return pltpu.make_async_remote_copy(
            src_ref=src, dst_ref=dst, send_sem=send, recv_sem=recv,
            device_id=dev, device_id_type=MESH)

    def lanes(unit, size):
        return pl.ds(pl.multiple_of(unit * size, size), size)

    loads = [pltpu.make_async_copy(k_hbm, kvin.at[0], ins.at[0]),
             pltpu.make_async_copy(v_hbm, kvin.at[1], ins.at[1]),
             pltpu.make_async_copy(q_hbm, qv, ins.at[2])]
    for load in loads:
        load.start()

    barrier = pltpu.get_barrier_semaphore()
    for d in range(1, nh):
        pl.semaphore_signal(barrier, inc=1, device_id=(s, (h + d) % nh), device_id_type=MESH)
    pl.semaphore_signal(barrier, inc=1, device_id=(y_peer, h), device_id_type=MESH)

    @pl.when(z < zsz - 1)
    def _():
        pl.semaphore_signal(barrier, inc=1, device_id=(s + ysz, h), device_id_type=MESH)

    @pl.when(z > 0)
    def _():
        pl.semaphore_signal(barrier, inc=1, device_id=(s - ysz, h), device_id_type=MESH)

    lane = lax.broadcasted_iota(jnp.int32, (1, 128), 1)
    info = jnp.zeros((1, 128), jnp.int32)
    for j in range(blk_seq):
        info = jnp.where(lane == j, own_slot_ref[j], info)
        for e in range(entries):
            block = jnp.where(e < cnt_ref[j], sel_ref[j, e], sel_ref[j, 0])
            info = jnp.where(lane == blk_seq + j * entries + e, block, info)
    rows_v[y, z] = info
    pair_rows = 2 * BLOCK_ROWS
    row = lax.rem(lax.broadcasted_iota(jnp.int32, (pair_rows, BLOCK_ROWS), 0), BLOCK_ROWS)
    col = lax.broadcasted_iota(jnp.int32, (pair_rows, BLOCK_ROWS), 1)
    diag[...] = jnp.where(col <= row, 0.0, -jnp.inf).astype(jnp.float32)
    vcat[:, HEAD_SIZE:] = jnp.ones((entries * BLOCK_ROWS, HEAD_SIZE), jnp.bfloat16)

    pl.semaphore_wait(barrier, nh + jnp.where(z < zsz - 1, 1, 0) + jnp.where(z > 0, 1, 0))

    def row_side(column):
        return remote(rows_v.at[column], rows_v.at[column], ss.at[0], sr.at[0], (y_peer, h))

    def row_up(t, zz, dev):
        ref = rows_v.at[y, zz]
        return remote(ref, ref, ss.at[1 + t], sr.at[1 + t], (dev, h))

    def row_down(t, zz, dev):
        ref = rows_v.at[y, zz]
        return remote(ref, ref, ss.at[1 + hops + t], sr.at[1 + hops + t], (dev, h))

    def head_near(g, role, place):
        return remote(kvin.at[role, :, lanes(side * heads + g, HEAD_SIZE)],
                      kv[g].at[role, z * nh + place],
                      hs.at[g, 0], hr.at[g, 0], (s, partner))

    def head_far(g, role):
        return remote(kvin.at[role, :, lanes((1 - side) * heads + g, HEAD_SIZE)],
                      kv[g].at[role, z * nh + h],
                      hs.at[g, 1 + role], hr.at[g, 1 + c], (s, (1 - side) * half + role))

    def head_far_in(g, spot):
        return remote(kvin.at[0, :, lanes(0, HEAD_SIZE)],
                      kv[g].at[c, z * nh + (1 - side) * half + spot],
                      hs.at[g, 1 + spot], hr.at[g, 1 + spot], (s, (1 - side) * half + spot))

    def q_head(g):
        return remote(qv.at[:, lanes((1 - side) * heads + g, width)], qbuf.at[g],
                      qs.at[g], qr.at[g], (s, x_peer))

    def part(g, zz, p):
        lo = (side + p) % 2 * half
        return kv[g].at[c, pl.ds(zz * nh + lo, half)]

    def up(g, p, t, zz, dev):
        ref = part(g, zz, p)
        return remote(ref, ref, us.at[g, p, t], ur.at[g, p, t], (dev, h))

    def down(g, p, t, zz, dev):
        ref = part(g, zz, p)
        return remote(ref, ref, ds_.at[g, p, t], dr.at[g, p, t], (dev, h))

    def across(g, r, zz):
        return remote(stage.at[g % 2, pl.ds(zz * PER_OWNER, PER_OWNER)],
                      kv[g].at[c, pl.ds(zsz * nh + zz * PER_OWNER, PER_OWNER)],
                      ys.at[g, r], yr.at[g, r], (y_peer, h))

    def share(g, r, zz, role):
        ref = kv[g].at[role, pl.ds(zz * nh, nh)]
        return remote(ref, ref, cs.at[g, 0, r], cr.at[g, 0, r], (s, partner))

    def share_far(g, r, zz, role):
        ref = kv[g].at[role, pl.ds(zsz * nh + zz * PER_OWNER, PER_OWNER)]
        return remote(ref, ref, cs.at[g, 1, r], cr.at[g, 1, r], (s, partner))

    def pass_on(g, r, zz):
        for k in range(PER_OWNER):
            pick = plan_s[k, r]
            chosen = kv[g][c, zz * nh + nh - 1]
            for j in reversed(range(nh - 1)):
                chosen = jnp.where(pick == j, kv[g][c, zz * nh + j], chosen)
            stage[g % 2, zz * PER_OWNER + k] = chosen
        across(g, r, zz).start()
        share(g, r, zz, c).start()

    def take_far(g, r, zz):
        across(g, r, zz).wait_recv()
        share_far(g, r, zz, c).start()

    def owners(t, call):
        @pl.when(z - 1 - t >= 0)
        def _():
            call(1 + t, z - 1 - t)

        @pl.when(z + 1 + t <= zsz - 1)
        def _():
            call(zsz + t, z + 1 + t)

    def every_owner(call):
        call(0, z)
        for t in range(zsz - 1):
            owners(t, call)

    def send_both(g, p):
        if zsz > 1:
            @pl.when(z < zsz - 1)
            def _():
                up(g, p, 0, z, s + ysz).start()

            @pl.when(z > 0)
            def _():
                down(g, p, 0, z, s - ysz).start()

    def open_near(g):
        head_near(g, c, partner).wait_recv()
        send_both(g, 0)

    def open_far(g):
        for spot in range(half):
            head_far_in(g, spot).wait_recv()
        send_both(g, 1)

    def open_z(g):
        open_near(g)
        open_far(g)

    def open_y(g):
        if g >= 2:
            every_owner(lambda r, zz: across(g - 2, r, zz).wait_send())
        pass_on(g, 0, z)

    def step(g, t):
        @pl.when(z - 1 - t >= 0)
        def _():
            below = z - 1 - t
            for p in range(2):
                up(g, p, t, below, s).wait_recv()
                if t + 1 < zsz - 1:
                    @pl.when(z < zsz - 1)
                    def _():
                        up(g, p, t + 1, below, s + ysz).start()

        @pl.when(z + 1 + t <= zsz - 1)
        def _():
            above = z + 1 + t
            for p in range(2):
                down(g, p, t, above, s).wait_recv()
                if t + 1 < zsz - 1:
                    @pl.when(z > 0)
                    def _():
                        down(g, p, t + 1, above, s - ysz).start()

    def side_step(g, t):
        owners(t, lambda r, zz: pass_on(g, r, zz))

    def take_step(g, t):
        if t < 0:
            take_far(g, 0, z)
        else:
            owners(t, lambda r, zz: take_far(g, r, zz))

    def close(g):
        every_owner(lambda r, zz: share(g, r, zz, 1 - c).wait_recv())
        every_owner(lambda r, zz: share_far(g, r, zz, 1 - c).wait_recv())

    def drain(g):
        head_near(g, 1 - c, h).wait_send()
        for role in range(2):
            head_far(g, role).wait_send()
        q_head(g).wait_send()
        if g + 2 >= heads:
            every_owner(lambda r, zz: across(g, r, zz).wait_send())
        every_owner(lambda r, zz: share(g, r, zz, c).wait_send())
        every_owner(lambda r, zz: share_far(g, r, zz, c).wait_send())
        for p in range(2):
            for t in range(zsz - 1):
                @pl.when((z < zsz - 1) & (z - t >= 0))
                def _():
                    up(g, p, t, z - t, s + ysz).wait_send()

                @pl.when((z > 0) & (z + t <= zsz - 1))
                def _():
                    down(g, p, t, z + t, s - ysz).wait_send()

    def share_rows():
        @pl.when(z < zsz - 1)
        def _():
            row_up(0, z, s + ysz).start()

        @pl.when(z > 0)
        def _():
            row_down(0, z, s - ysz).start()

    def gather_rows(t):
        @pl.when(z - 1 - t >= 0)
        def _():
            row_up(t, z - 1 - t, s).wait_recv()
            if t + 1 < zsz - 1:
                @pl.when(z < zsz - 1)
                def _():
                    row_up(t + 1, z - 1 - t, s + ysz).start()

        @pl.when(z + 1 + t <= zsz - 1)
        def _():
            row_down(t, z + 1 + t, s).wait_recv()
            if t + 1 < zsz - 1:
                @pl.when(z > 0)
                def _():
                    row_down(t + 1, z + 1 + t, s - ysz).start()

    def drain_rows():
        row_side(y).wait_send()
        for t in range(zsz - 1):
            @pl.when((z < zsz - 1) & (z - t >= 0))
            def _():
                row_up(t, z - t, s + ysz).wait_send()

            @pl.when((z > 0) & (z + t <= zsz - 1))
            def _():
                row_down(t, z + t, s - ysz).wait_send()

    def slot_of(column, place, i):
        b = rows_s[column, place, 0, blk_seq + i]
        home = lax.div(b, blk_seq)
        slot = rows_s[lax.rem(home, ysz), lax.div(home, ysz), 0, lax.rem(b, blk_seq)]
        owner = lax.div(slot, nh)
        return lax.rem(slot, nh), lax.div(owner, ysz), lax.rem(owner, ysz)

    def plan_send():
        row_side(1 - y).wait_recv()
        table = pltpu.make_async_copy(rows_v, rows_s, local_sem)
        table.start()
        table.wait()
        first = jnp.full((1, 128), nh, jnp.int32)
        last = jnp.full((1, 128), -1, jnp.int32)
        for i in range(blk_seq * entries):
            j, oz, oy = slot_of(1 - y, z, i)
            r = jnp.where(oz < z, z - oz, jnp.where(oz > z, zsz - 1 + oz - z, 0))
            hit = lane == jnp.where(oy == y, r, -1)
            first = jnp.where(hit, jnp.minimum(first, j), first)
            last = jnp.where(hit, jnp.maximum(last, j), last)
        plan_v[0:1, :] = first
        plan_v[1:2, :] = last
        copy = pltpu.make_async_copy(plan_v, plan_s, local_sem)
        copy.start()
        copy.wait()

    def plan_fetch():
        mine = [slot_of(y, z, i) for i in range(blk_seq * entries)]
        js = jnp.zeros((1, 128), jnp.int32)
        ozs = jnp.zeros((1, 128), jnp.int32)
        oys = jnp.zeros((1, 128), jnp.int32)
        for i, (j, oz, oy) in enumerate(mine):
            js = jnp.where(lane == i, j, js)
            ozs = jnp.where(lane == i, oz, ozs)
            oys = jnp.where(lane == i, oy, oys)
        second = jnp.zeros((1, 128), jnp.int32)
        for j, oz, oy in mine:
            second = jnp.where((ozs == oz) & (oys == oy) & (js > j), 1, second)
        place = jnp.where(oys == y, ozs * nh + js, zsz * nh + ozs * PER_OWNER + second)
        place_v[0:1, :] = place
        copy = pltpu.make_async_copy(place_v, place_s, local_sem)
        copy.start()
        copy.wait()

    factor = math.log2(math.e) / math.sqrt(HEAD_SIZE)

    def fetch(g, j):
        for e in range(entries):
            place = place_s[0, j * entries + e]
            rows = slice(e * BLOCK_ROWS, (e + 1) * BLOCK_ROWS)
            kcat[rows, :] = kv[g][0, place]
            vcat[rows, :HEAD_SIZE] = kv[g][1, place]

    def bias_of(j):
        rest = lax.broadcasted_iota(jnp.int32, (1, (entries - 1) * BLOCK_ROWS), 1) + BLOCK_ROWS
        return jnp.where(rest < cnt_ref[j] * BLOCK_ROWS, 0.0, -jnp.inf).astype(jnp.float32)

    def pair(q2, bias):
        q2 = jnp.concatenate([q2[:, :HEAD_SIZE], q2[:, HEAD_SIZE:]], axis=0)
        scores = lax.dot_general(q2, kcat[...], (((1,), (1,)), ((), ())),
                                 preferred_element_type=jnp.float32)
        own = scores[:, :BLOCK_ROWS] + diag[...]
        others = scores[:, BLOCK_ROWS:] + bias
        scores = jnp.concatenate([own, others], axis=1)
        top = jnp.max(scores, axis=1, keepdims=True)
        weights = jnp.exp2((scores - top) * factor).astype(jnp.bfloat16)
        mixed = jnp.dot(weights, vcat[...], preferred_element_type=jnp.float32)
        result = (mixed[:, :HEAD_SIZE] / mixed[:, HEAD_SIZE:]).astype(jnp.bfloat16)
        return jnp.concatenate([result[:BLOCK_ROWS], result[BLOCK_ROWS:]], axis=1)

    span = 2 * HEAD_SIZE

    def result_out(g, i):
        return remote(obuf.at[g, :, pl.ds(i * span, span)],
                      out_ref.at[:, lanes((side * heads + g) * pairs + i, span)],
                      os_.at[g, i], or_.at[g, i], (s, x_peer))

    def result_in(g, i):
        return remote(obuf.at[g, :, pl.ds(i * span, span)],
                      out_ref.at[:, lanes(((1 - side) * heads + g) * pairs + i, span)],
                      os_.at[g, i], or_.at[g, i], (s, x_peer))

    share_rows()
    loads[0].wait()
    loads[1].wait()
    for g in range(heads):
        head_near(g, 1 - c, h).start()
        for role in range(2):
            head_far(g, role).start()
        kv[g][c, z * nh + h] = kvin[c, :, lanes(side * heads + g, HEAD_SIZE)]
    loads[2].wait()
    for g in range(heads):
        q_head(g).start()
    last = zsz - 2
    open_near(0)
    gather_rows(0)
    open_far(0)
    for t in range(1, zsz - 1):
        gather_rows(t)
    row_side(y).start()
    open_z(1)
    step(0, 0)
    plan_send()
    open_y(0)
    side_step(0, 0)
    for t in range(1, last):
        step(0, t)
        side_step(0, t)
    open_z(2)
    plan_fetch()

    def far_query(g):
        fetch(g, x_peer)
        bias = bias_of(x_peer)
        q_head(g).wait_recv()
        for i in range(pairs):
            obuf[g, :, i * span:(i + 1) * span] = pair(qbuf[g, :, i * span:(i + 1) * span], bias)
            if g + 1 == heads and i > 0:
                result_out(g, i - 1).start()
        for i in range(pairs - 1 if g + 1 == heads else 0, pairs):
            result_out(g, i).start()

    def own_query(g):
        fetch(g, h)
        bias = bias_of(h)
        for i in range(pairs):
            cols = lanes((side * heads + g) * pairs + i, span)
            out_ref[:, cols] = pair(qv[:, cols], bias)

    for g in range(heads):
        more = g + 1 < heads
        step(g, last)
        side_step(g, last)
        if g > 0:
            own_query(g - 1)
        if more:
            step(g + 1, 0)
            open_y(g + 1)
            side_step(g + 1, 0)
        for t in range(-1, zsz - 1):
            take_step(g, t)
        if more:
            for t in range(1, last):
                step(g + 1, t)
                side_step(g + 1, t)
            if g + 3 < heads:
                open_z(g + 3)
        close(g)
        far_query(g)
    own_query(heads - 1)

    for g in range(heads):
        drain(g)
    drain_rows()
    for g in range(heads):
        for i in range(pairs):
            result_out(g, i).wait_send()
            result_in(g, i).wait_recv()


def body(queries, keys, values, selected, counts, block_slot):
    ns = lax.axis_size("seq")
    nh = lax.axis_size("head")
    blk_seq, entries = selected.shape
    rows = queries.shape[0]
    heads = keys.shape[1] // HEAD_SIZE // 2
    width = queries.shape[1] // 2 // heads
    assert rows == BLOCK_ROWS and blk_seq == nh and nh == 4
    assert ns % Y_SIZE == 0 and ns > 2 * Y_SIZE and heads > 2
    hbm = pl.BlockSpec(memory_space=pl.ANY)
    smem = pl.BlockSpec(memory_space=pltpu.SMEM)
    zsz = ns // Y_SIZE
    dma = pltpu.SemaphoreType.DMA
    hops = max(zsz - 1, 1)
    held = zsz * (nh + PER_OWNER)
    pairs = width // (2 * HEAD_SIZE)
    big = [pltpu.with_memory_space_constraint(a, pltpu.HBM) for a in (queries, keys, values)]
    return pl.pallas_call(
        functools.partial(kernel, ns, nh, heads, entries),
        out_shape=pltpu.VMEM(queries.shape, jnp.bfloat16),
        in_specs=[hbm, hbm, hbm, smem, smem, smem],
        out_specs=pl.BlockSpec(memory_space=pltpu.VMEM),
        scratch_shapes=[
            pltpu.VMEM(queries.shape, jnp.bfloat16),
            pltpu.VMEM((2,) + keys.shape, jnp.bfloat16),
            pltpu.VMEM((heads, rows, width), jnp.bfloat16),
            pltpu.VMEM((heads, rows, width), jnp.bfloat16),
            pltpu.VMEM((entries * BLOCK_ROWS, HEAD_SIZE), jnp.bfloat16),
            pltpu.VMEM((entries * BLOCK_ROWS, 2 * HEAD_SIZE), jnp.bfloat16),
            pltpu.VMEM((2 * BLOCK_ROWS, BLOCK_ROWS), jnp.float32),
            pltpu.VMEM((2, zsz * PER_OWNER, BLOCK_ROWS, HEAD_SIZE), jnp.bfloat16),
            pltpu.VMEM((Y_SIZE, zsz, 1, 128), jnp.int32),
            pltpu.SMEM((Y_SIZE, zsz, 1, 128), jnp.int32),
            pltpu.VMEM((8, 128), jnp.int32),
            pltpu.SMEM((8, 128), jnp.int32),
            pltpu.VMEM((8, 128), jnp.int32),
            pltpu.SMEM((8, 128), jnp.int32),
            dma((3,)), dma,
            dma((heads, 3)), dma((heads, 3)),
            dma((heads,)), dma((heads,)),
            dma((heads, 2, hops)), dma((heads, 2, hops)),
            dma((heads, 2, hops)), dma((heads, 2, hops)),
            dma((heads, 2 * zsz)), dma((heads, 2 * zsz)),
            dma((heads, 2, 2 * zsz)), dma((heads, 2, 2 * zsz)),
            dma((heads, pairs)), dma((heads, pairs)),
            dma((1 + 2 * hops,)), dma((1 + 2 * hops,)),
        ] + [pltpu.VMEM((2, held, BLOCK_ROWS, HEAD_SIZE), jnp.bfloat16)] * heads,
        compiler_params=pltpu.CompilerParams(
            collective_id=0, has_side_effects=True, vmem_limit_bytes=60 * 1024 * 1024),
        name="block_attention",
    )(*big, selected, counts, block_slot)


def solution(mesh):
    return jax.shard_map(
        body,
        mesh=mesh,
        in_specs=(
            P(("seq", "head"), None),
            P(("seq", "head"), None),
            P(("seq", "head"), None),
            P("seq", None),
            P("seq"),
            P("seq"),
        ),
        out_specs=P(("seq", "head"), None),
        check_vma=False,
    )
```

time: 71.4 us -> 63.2 us (0.89)
  Pallas kernels: 67.9 us -> 61.8 us
  local copies, waits for them, and re-layouts: 3.1 us -> 1.32 us
    pallas_call x1, Pallas kernels: 67.9 us -> 61.8 us  [body(): pl.pallas_call(functools.partial(kernel, ns, nh, heads, entries), out_sha...]
    unnamed x1, local copies, waits for them, and re-layouts: 3.1 us -> 1.32 us
where the time goes in v2:
time: 63.2 us; the launch traced here: 63.1 us
  Pallas kernels  61.8 us (98%)
  local copies, waits for them, and re-layouts  1.32 us (2%)
    pallas_call x1, Pallas kernels, body(): pl.pallas_call(functools.partial(kernel, ns, nh, heads, entries), out_sha...  61.8 us
    unnamed x1, local copies, waits for them, and re-layouts  1.32 us

profile of v2, /device:TPU:0, one launch (start us, length us, event | category | flops | bytes accessed | tf_op | source)
XLA Modules:
  0.0 63.1 jit_solution(9377134305463775347)
XLA Ops:
  0.0 61.8 %block_attention.1 = bf16[128,8192]{1,0:T(8,128)(2,1)S(1)} custom-call(bf16[128,8192]{1,0:T(8,128)(2,1)} %q_hbm.1, bf16[128,1024]{1,0:T(8,128)(2,1)} %k_hbm.1, bf16[128,1024]{1,0:T(8,128)(2,1)} %v_hbm.1, s32[4,8]{1,0:T(4,128)} %sel_ref.1, s32[4]{0:T(128)} %cnt_ref.1, s32[4]{0:T(128)} %own_slot_ref.1), custom_call_target="tpu_custom_call" | custom-call | tf_op jit(solution)/shard_map/block_attention/pallas_call | solution.py:461
  61.8 1.3 %copy.8 = bf16[128,8192]{1,0:T(8,128)(2,1)} copy(bf16[128,8192]{1,0:T(8,128)(2,1)S(1)} %block_attention.1) | data formatting | bytes 4194304

commit v3 on v2

--- a/solution.py
+++ b/solution.py
@@ -25,6 +25,7 @@
     ysz = Y_SIZE
     zsz = ns // ysz
     hops = max(zsz - 1, 1)
+    held = zsz * (nh + PER_OWNER)
     z = s // ysz
     y = s % ysz
     y_peer = s + 1 - 2 * y
@@ -94,21 +95,24 @@
     def head_near(g, role, place):
         return remote(kvin.at[role, :, lanes(side * heads + g, HEAD_SIZE)],
                       kv[g].at[role, z * nh + place],
-                      hs.at[g, 0], hr.at[g, 0], (s, partner))
+                      hs.at[g], hr.at[g, 0], (s, partner))
 
     def head_far(g, role):
         return remote(kvin.at[role, :, lanes((1 - side) * heads + g, HEAD_SIZE)],
                       kv[g].at[role, z * nh + h],
-                      hs.at[g, 1 + role], hr.at[g, 1 + c], (s, (1 - side) * half + role))
-
-    def head_far_in(g, spot):
-        return remote(kvin.at[0, :, lanes(0, HEAD_SIZE)],
-                      kv[g].at[c, z * nh + (1 - side) * half + spot],
-                      hs.at[g, 1 + spot], hr.at[g, 1 + spot], (s, (1 - side) * half + spot))
+                      hs.at[g], hr.at[g, 1], (s, (1 - side) * half + role))
+
+    def head_far_in(g):
+        ref = kv[g].at[c, pl.ds(z * nh + (1 - side) * half, half)]
+        return remote(ref, ref, hs.at[g], hr.at[g, 1], (s, x_peer))
+
+    def head_sent(g):
+        ref = kv[g].at[0, pl.ds(0, nh - 1)]
+        return remote(ref, ref, hs.at[g], hr.at[g, 1], (s, x_peer))
 
     def q_head(g):
         return remote(qv.at[:, lanes((1 - side) * heads + g, width)], qbuf.at[g],
-                      qs.at[g], qr.at[g], (s, x_peer))
+                      qs, qr.at[g], (s, x_peer))
 
     def part(g, zz, p):
         lo = (side + p) % 2 * half
@@ -116,24 +120,28 @@
 
     def up(g, p, t, zz, dev):
         ref = part(g, zz, p)
-        return remote(ref, ref, us.at[g, p, t], ur.at[g, p, t], (dev, h))
+        return remote(ref, ref, us.at[g], ur.at[g, p, t], (dev, h))
 
     def down(g, p, t, zz, dev):
         ref = part(g, zz, p)
-        return remote(ref, ref, ds_.at[g, p, t], dr.at[g, p, t], (dev, h))
-
-    def across(g, r, zz):
-        return remote(stage.at[g % 2, pl.ds(zz * PER_OWNER, PER_OWNER)],
-                      kv[g].at[c, pl.ds(zsz * nh + zz * PER_OWNER, PER_OWNER)],
-                      ys.at[g, r], yr.at[g, r], (y_peer, h))
-
-    def share(g, r, zz, role):
-        ref = kv[g].at[role, pl.ds(zz * nh, nh)]
-        return remote(ref, ref, cs.at[g, 0, r], cr.at[g, 0, r], (s, partner))
-
-    def share_far(g, r, zz, role):
-        ref = kv[g].at[role, pl.ds(zsz * nh + zz * PER_OWNER, PER_OWNER)]
-        return remote(ref, ref, cs.at[g, 1, r], cr.at[g, 1, r], (s, partner))
+        return remote(ref, ref, ds_.at[g], dr.at[g, p, t], (dev, h))
+
+    def ups(g, count):
+        ref = kv[g].at[c, pl.ds(0, count * nh)]
+        return remote(ref, ref, us.at[g], ur.at[g, 0, 0], (s, h))
+
+    def downs(g, count):
+        ref = kv[g].at[c, pl.ds((zsz - count) * nh, count * nh)]
+        return remote(ref, ref, ds_.at[g], dr.at[g, 0, 0], (s, h))
+
+    def across(g, zz, count):
+        return remote(stage.at[g % 2, pl.ds(zz * PER_OWNER, count * PER_OWNER)],
+                      kv[g].at[c, pl.ds(zsz * nh + zz * PER_OWNER, count * PER_OWNER)],
+                      ys.at[g], yr.at[g], (y_peer, h))
+
+    def share(g, start, size, role):
+        ref = kv[g].at[role, pl.ds(start, size)]
+        return remote(ref, ref, cs.at[g], cr.at[g], (s, partner))
 
     def pass_on(g, r, zz):
         for k in range(PER_OWNER):
@@ -142,12 +150,12 @@
             for j in reversed(range(nh - 1)):
                 chosen = jnp.where(pick == j, kv[g][c, zz * nh + j], chosen)
             stage[g % 2, zz * PER_OWNER + k] = chosen
-        across(g, r, zz).start()
-        share(g, r, zz, c).start()
-
-    def take_far(g, r, zz):
-        across(g, r, zz).wait_recv()
-        share_far(g, r, zz, c).start()
+        across(g, zz, 1).start()
+        share(g, zz * nh, nh, c).start()
+
+    def take_far(g):
+        across(g, 0, zsz).wait_recv()
+        share(g, zsz * nh, zsz * PER_OWNER, c).start()
 
     def owners(t, call):
         @pl.when(z - 1 - t >= 0)
@@ -157,11 +165,6 @@
         @pl.when(z + 1 + t <= zsz - 1)
         def _():
             call(zsz + t, z + 1 + t)
-
-    def every_owner(call):
-        call(0, z)
-        for t in range(zsz - 1):
-            owners(t, call)
 
     def send_both(g, p):
         if zsz > 1:
@@ -178,8 +181,7 @@
         send_both(g, 0)
 
     def open_far(g):
-        for spot in range(half):
-            head_far_in(g, spot).wait_recv()
+        head_far_in(g).wait_recv()
         send_both(g, 1)
 
     def open_z(g):
@@ -188,61 +190,46 @@
 
     def open_y(g):
         if g >= 2:
-            every_owner(lambda r, zz: across(g - 2, r, zz).wait_send())
+            across(g - 2, 0, zsz).wait_send()
         pass_on(g, 0, z)
 
     def step(g, t):
-        @pl.when(z - 1 - t >= 0)
-        def _():
-            below = z - 1 - t
-            for p in range(2):
-                up(g, p, t, below, s).wait_recv()
+        for p in range(2):
+            @pl.when(z - 1 - t >= 0)
+            def _():
+                up(g, p, t, z - 1 - t, s).wait_recv()
                 if t + 1 < zsz - 1:
                     @pl.when(z < zsz - 1)
                     def _():
-                        up(g, p, t + 1, below, s + ysz).start()
-
-        @pl.when(z + 1 + t <= zsz - 1)
-        def _():
-            above = z + 1 + t
-            for p in range(2):
-                down(g, p, t, above, s).wait_recv()
+                        up(g, p, t + 1, z - 1 - t, s + ysz).start()
+
+            @pl.when(z + 1 + t <= zsz - 1)
+            def _():
+                down(g, p, t, z + 1 + t, s).wait_recv()
                 if t + 1 < zsz - 1:
                     @pl.when(z > 0)
                     def _():
-                        down(g, p, t + 1, above, s - ysz).start()
+                        down(g, p, t + 1, z + 1 + t, s - ysz).start()
 
     def side_step(g, t):
         owners(t, lambda r, zz: pass_on(g, r, zz))
 
-    def take_step(g, t):
-        if t < 0:
-            take_far(g, 0, z)
-        else:
-            owners(t, lambda r, zz: take_far(g, r, zz))
-
     def close(g):
-        every_owner(lambda r, zz: share(g, r, zz, 1 - c).wait_recv())
-        every_owner(lambda r, zz: share_far(g, r, zz, 1 - c).wait_recv())
+        share(g, 0, held, 1 - c).wait_recv()
 
     def drain(g):
-        head_near(g, 1 - c, h).wait_send()
-        for role in range(2):
-            head_far(g, role).wait_send()
-        q_head(g).wait_send()
+        head_sent(g).wait_send()
         if g + 2 >= heads:
-            every_owner(lambda r, zz: across(g, r, zz).wait_send())
-        every_owner(lambda r, zz: share(g, r, zz, c).wait_send())
-        every_owner(lambda r, zz: share_far(g, r, zz, c).wait_send())
-        for p in range(2):
-            for t in range(zsz - 1):
-                @pl.when((z < zsz - 1) & (z - t >= 0))
-                def _():
-                    up(g, p, t, z - t, s + ysz).wait_send()
-
-                @pl.when((z > 0) & (z + t <= zsz - 1))
-                def _():
-                    down(g, p, t, z + t, s - ysz).wait_send()
+            across(g, 0, zsz).wait_send()
+        share(g, 0, held, c).wait_send()
+        for count in range(1, zsz):
+            @pl.when(z == count - 1)
+            def _():
+                ups(g, count).wait_send()
+
+            @pl.when(z == zsz - count)
+            def _():
+                downs(g, count).wait_send()
 
     def share_rows():
         @pl.when(z < zsz - 1)
@@ -353,15 +340,15 @@
 
     span = 2 * HEAD_SIZE
 
-    def result_out(g, i):
-        return remote(obuf.at[g, :, pl.ds(i * span, span)],
-                      out_ref.at[:, lanes((side * heads + g) * pairs + i, span)],
-                      os_.at[g, i], or_.at[g, i], (s, x_peer))
-
-    def result_in(g, i):
-        return remote(obuf.at[g, :, pl.ds(i * span, span)],
-                      out_ref.at[:, lanes(((1 - side) * heads + g) * pairs + i, span)],
-                      os_.at[g, i], or_.at[g, i], (s, x_peer))
+    def result_out(g, i, size):
+        cols = pl.ds((side * heads + g) * width + i * size, size)
+        cols = pl.ds(pl.multiple_of(cols.start, size), size)
+        return remote(obuf.at[g, :, pl.ds(i * size, size)], out_ref.at[:, cols],
+                      os_, or_, (s, x_peer))
+
+    def results():
+        cols = lanes(1 - side, heads * width)
+        return remote(qv.at[:, cols], out_ref.at[:, cols], os_, or_, (s, x_peer))
 
     share_rows()
     loads[0].wait()
@@ -377,19 +364,20 @@
     last = zsz - 2
     open_near(0)
     gather_rows(0)
+    open_near(1)
     open_far(0)
     for t in range(1, zsz - 1):
         gather_rows(t)
     row_side(y).start()
-    open_z(1)
+    open_far(1)
     step(0, 0)
+    open_z(2)
     plan_send()
     open_y(0)
     side_step(0, 0)
     for t in range(1, last):
         step(0, t)
         side_step(0, t)
-    open_z(2)
     plan_fetch()
 
     def far_query(g):
@@ -399,9 +387,11 @@
         for i in range(pairs):
             obuf[g, :, i * span:(i + 1) * span] = pair(qbuf[g, :, i * span:(i + 1) * span], bias)
             if g + 1 == heads and i > 0:
-                result_out(g, i - 1).start()
-        for i in range(pairs - 1 if g + 1 == heads else 0, pairs):
-            result_out(g, i).start()
+                result_out(g, i - 1, span).start()
+        if g + 1 == heads:
+            result_out(g, pairs - 1, span).start()
+        else:
+            result_out(g, 0, width).start()
 
     def own_query(g):
         fetch(g, h)
@@ -416,18 +406,17 @@
         side_step(g, last)
         if g > 0:
             own_query(g - 1)
+        if g + 3 < heads:
+            open_z(g + 3)
         if more:
             step(g + 1, 0)
             open_y(g + 1)
             side_step(g + 1, 0)
-        for t in range(-1, zsz - 1):
-            take_step(g, t)
+        take_far(g)
         if more:
             for t in range(1, last):
                 step(g + 1, t)
                 side_step(g + 1, t)
-            if g + 3 < heads:
-                open_z(g + 3)
         close(g)
         far_query(g)
     own_query(heads - 1)
@@ -435,10 +424,9 @@
     for g in range(heads):
         drain(g)
     drain_rows()
-    for g in range(heads):
-        for i in range(pairs):
-            result_out(g, i).wait_send()
-            result_in(g, i).wait_recv()
+    remote(qbuf, qbuf, qs, qr.at[0], (s, x_peer)).wait_send()
+    results().wait_send()
+    results().wait_recv()
 
 
 def body(queries, keys, values, selected, counts, block_slot):
@@ -456,7 +444,6 @@
     dma = pltpu.SemaphoreType.DMA
     hops = max(zsz - 1, 1)
     held = zsz * (nh + PER_OWNER)
-    pairs = width // (2 * HEAD_SIZE)
     big = [pltpu.with_memory_space_constraint(a, pltpu.HBM) for a in (queries, keys, values)]
     return pl.pallas_call(
         functools.partial(kernel, ns, nh, heads, entries),
@@ -479,13 +466,13 @@
             pltpu.VMEM((8, 128), jnp.int32),
             pltpu.SMEM((8, 128), jnp.int32),
             dma((3,)), dma,
-            dma((heads, 3)), dma((heads, 3)),
+            dma((heads,)), dma((heads, 2)),
+            dma, dma((heads,)),
+            dma((heads,)), dma((heads, 2, hops)),
+            dma((heads,)), dma((heads, 2, hops)),
             dma((heads,)), dma((heads,)),
-            dma((heads, 2, hops)), dma((heads, 2, hops)),
-            dma((heads, 2, hops)), dma((heads, 2, hops)),
-            dma((heads, 2 * zsz)), dma((heads, 2 * zsz)),
-            dma((heads, 2, 2 * zsz)), dma((heads, 2, 2 * zsz)),
-            dma((heads, pairs)), dma((heads, pairs)),
+            dma((heads,)), dma((heads,)),
+            dma, dma,
             dma((1 + 2 * hops,)), dma((1 + 2 * hops,)),
         ] + [pltpu.VMEM((2, held, BLOCK_ROWS, HEAD_SIZE), jnp.bfloat16)] * heads,
         compiler_params=pltpu.CompilerParams(

time: 63.2 us -> 59.3 us (0.938)
  Pallas kernels: 61.8 us -> 57.8 us
    pallas_call x1, Pallas kernels: 61.8 us -> 57.8 us  [body(): pl.pallas_call(functools.partial(kernel, ns, nh, heads, entries), out_sha...]
where the time goes in v3:
time: 59.3 us; the launch traced here: 59.1 us
  Pallas kernels  57.8 us (97%)
  local copies, waits for them, and re-layouts  1.32 us (2%)
    pallas_call x1, Pallas kernels, body(): pl.pallas_call(functools.partial(kernel, ns, nh, heads, entries), out_sha...  57.8 us
    unnamed x1, local copies, waits for them, and re-layouts  1.32 us

profile of v3, /device:TPU:0, one launch (start us, length us, event | category | flops | bytes accessed | tf_op | source)
XLA Modules:
  0.0 59.1 jit_solution(12720235435139492303)
XLA Ops:
  0.0 57.8 %block_attention.1 = bf16[128,8192]{1,0:T(8,128)(2,1)S(1)} custom-call(bf16[128,8192]{1,0:T(8,128)(2,1)} %q_hbm.1, bf16[128,1024]{1,0:T(8,128)(2,1)} %k_hbm.1, bf16[128,1024]{1,0:T(8,128)(2,1)} %v_hbm.1, s32[4,8]{1,0:T(4,128)} %sel_ref.1, s32[4]{0:T(128)} %cnt_ref.1, s32[4]{0:T(128)} %own_slot_ref.1), custom_call_target="tpu_custom_call" | custom-call | tf_op jit(solution)/shard_map/block_attention/pallas_call | solution.py:448
  57.8 1.3 %copy.8 = bf16[128,8192]{1,0:T(8,128)(2,1)} copy(bf16[128,8192]{1,0:T(8,128)(2,1)S(1)} %block_attention.1) | data formatting | bytes 4194304

commit v4 on v3

--- a/solution.py
+++ b/solution.py
@@ -17,7 +17,8 @@
 MESH = pl.DeviceIdType.MESH
 
 
-def kernel(ns, nh, heads, entries, q_hbm, k_hbm, v_hbm, sel_ref, cnt_ref, own_slot_ref, out_ref,
+def kernel(ns, nh, heads, entries, q_hbm, k_hbm, v_hbm, sel_hbm, cnt_hbm, slot_hbm, out_ref,
+           sel_ref, cnt_ref, own_slot_ref,
            qv, kvin, qbuf, obuf, kcat, vcat, diag, stage, rows_v, rows_s, plan_v, plan_s, place_v, place_s,
            ins, local_sem, hs, hr, qs, qr, us, ur, ds_, dr, ys, yr, cs, cr, os_, or_, ss, sr, *kv):
     s = lax.axis_index("seq")
@@ -46,26 +47,36 @@
     def lanes(unit, size):
         return pl.ds(pl.multiple_of(unit * size, size), size)
 
-    loads = [pltpu.make_async_copy(k_hbm, kvin.at[0], ins.at[0]),
+    barrier = pltpu.get_barrier_semaphore()
+    for d in range(1, nh):
+        pl.semaphore_signal(barrier, inc=1, device_id=(s, (h + d) % nh), device_id_type=MESH)
+    pl.semaphore_signal(barrier, inc=1, device_id=(y_peer, h), device_id_type=MESH)
+
+    @pl.when(z < zsz - 1)
+    def _():
+        pl.semaphore_signal(barrier, inc=1, device_id=(s + ysz, h), device_id_type=MESH)
+
+    @pl.when(z > 0)
+    def _():
+        pl.semaphore_signal(barrier, inc=1, device_id=(s - ysz, h), device_id_type=MESH)
+
+    loads = [pltpu.make_async_copy(sel_hbm, sel_ref, ins.at[3]),
+             pltpu.make_async_copy(cnt_hbm, cnt_ref, ins.at[4]),
+             pltpu.make_async_copy(slot_hbm, own_slot_ref, ins.at[5]),
+             pltpu.make_async_copy(k_hbm, kvin.at[0], ins.at[0]),
              pltpu.make_async_copy(v_hbm, kvin.at[1], ins.at[1]),
              pltpu.make_async_copy(q_hbm, qv, ins.at[2])]
     for load in loads:
         load.start()
 
-    barrier = pltpu.get_barrier_semaphore()
-    for d in range(1, nh):
-        pl.semaphore_signal(barrier, inc=1, device_id=(s, (h + d) % nh), device_id_type=MESH)
-    pl.semaphore_signal(barrier, inc=1, device_id=(y_peer, h), device_id_type=MESH)
-
-    @pl.when(z < zsz - 1)
-    def _():
-        pl.semaphore_signal(barrier, inc=1, device_id=(s + ysz, h), device_id_type=MESH)
-
-    @pl.when(z > 0)
-    def _():
-        pl.semaphore_signal(barrier, inc=1, device_id=(s - ysz, h), device_id_type=MESH)
-
     lane = lax.broadcasted_iota(jnp.int32, (1, 128), 1)
+    pair_rows = 2 * BLOCK_ROWS
+    row = lax.rem(lax.broadcasted_iota(jnp.int32, (pair_rows, BLOCK_ROWS), 0), BLOCK_ROWS)
+    col = lax.broadcasted_iota(jnp.int32, (pair_rows, BLOCK_ROWS), 1)
+    diag[...] = jnp.where(col <= row, 0.0, -jnp.inf).astype(jnp.float32)
+    vcat[:, HEAD_SIZE:] = jnp.ones((entries * BLOCK_ROWS, HEAD_SIZE), jnp.bfloat16)
+    for load in loads[:3]:
+        load.wait()
     info = jnp.zeros((1, 128), jnp.int32)
     for j in range(blk_seq):
         info = jnp.where(lane == j, own_slot_ref[j], info)
@@ -73,11 +84,6 @@
             block = jnp.where(e < cnt_ref[j], sel_ref[j, e], sel_ref[j, 0])
             info = jnp.where(lane == blk_seq + j * entries + e, block, info)
     rows_v[y, z] = info
-    pair_rows = 2 * BLOCK_ROWS
-    row = lax.rem(lax.broadcasted_iota(jnp.int32, (pair_rows, BLOCK_ROWS), 0), BLOCK_ROWS)
-    col = lax.broadcasted_iota(jnp.int32, (pair_rows, BLOCK_ROWS), 1)
-    diag[...] = jnp.where(col <= row, 0.0, -jnp.inf).astype(jnp.float32)
-    vcat[:, HEAD_SIZE:] = jnp.ones((entries * BLOCK_ROWS, HEAD_SIZE), jnp.bfloat16)
 
     pl.semaphore_wait(barrier, nh + jnp.where(z < zsz - 1, 1, 0) + jnp.where(z > 0, 1, 0))
 
@@ -351,27 +357,28 @@
         return remote(qv.at[:, cols], out_ref.at[:, cols], os_, or_, (s, x_peer))
 
     share_rows()
-    loads[0].wait()
-    loads[1].wait()
+    loads[3].wait()
+    loads[4].wait()
     for g in range(heads):
         head_near(g, 1 - c, h).start()
         for role in range(2):
             head_far(g, role).start()
         kv[g][c, z * nh + h] = kvin[c, :, lanes(side * heads + g, HEAD_SIZE)]
-    loads[2].wait()
+    loads[5].wait()
     for g in range(heads):
         q_head(g).start()
     last = zsz - 2
     open_near(0)
     gather_rows(0)
     open_near(1)
+    open_near(2)
     open_far(0)
     for t in range(1, zsz - 1):
         gather_rows(t)
     row_side(y).start()
     open_far(1)
     step(0, 0)
-    open_z(2)
+    open_far(2)
     plan_send()
     open_y(0)
     side_step(0, 0)
@@ -386,10 +393,10 @@
         q_head(g).wait_recv()
         for i in range(pairs):
             obuf[g, :, i * span:(i + 1) * span] = pair(qbuf[g, :, i * span:(i + 1) * span], bias)
-            if g + 1 == heads and i > 0:
-                result_out(g, i - 1, span).start()
+            if g + 1 == heads and i == pairs // 2:
+                result_out(g, 0, width // 2).start()
         if g + 1 == heads:
-            result_out(g, pairs - 1, span).start()
+            result_out(g, 1, width // 2).start()
         else:
             result_out(g, 0, width).start()
 
@@ -404,12 +411,13 @@
         more = g + 1 < heads
         step(g, last)
         side_step(g, last)
-        if g > 0:
-            own_query(g - 1)
         if g + 3 < heads:
             open_z(g + 3)
         if more:
             step(g + 1, 0)
+        if g > 0:
+            own_query(g - 1)
+        if more:
             open_y(g + 1)
             side_step(g + 1, 0)
         take_far(g)
@@ -439,18 +447,21 @@
     assert rows == BLOCK_ROWS and blk_seq == nh and nh == 4
     assert ns % Y_SIZE == 0 and ns > 2 * Y_SIZE and heads > 2
     hbm = pl.BlockSpec(memory_space=pl.ANY)
-    smem = pl.BlockSpec(memory_space=pltpu.SMEM)
     zsz = ns // Y_SIZE
     dma = pltpu.SemaphoreType.DMA
     hops = max(zsz - 1, 1)
     held = zsz * (nh + PER_OWNER)
-    big = [pltpu.with_memory_space_constraint(a, pltpu.HBM) for a in (queries, keys, values)]
+    big = [pltpu.with_memory_space_constraint(a, pltpu.HBM)
+           for a in (queries, keys, values, selected, counts, block_slot)]
     return pl.pallas_call(
         functools.partial(kernel, ns, nh, heads, entries),
         out_shape=pltpu.VMEM(queries.shape, jnp.bfloat16),
-        in_specs=[hbm, hbm, hbm, smem, smem, smem],
+        in_specs=[hbm] * 6,
         out_specs=pl.BlockSpec(memory_space=pltpu.VMEM),
         scratch_shapes=[
+            pltpu.SMEM(selected.shape, jnp.int32),
+            pltpu.SMEM(counts.shape, jnp.int32),
+            pltpu.SMEM(block_slot.shape, jnp.int32),
             pltpu.VMEM(queries.shape, jnp.bfloat16),
             pltpu.VMEM((2,) + keys.shape, jnp.bfloat16),
             pltpu.VMEM((heads, rows, width), jnp.bfloat16),
@@ -465,7 +476,7 @@
             pltpu.SMEM((8, 128), jnp.int32),
             pltpu.VMEM((8, 128), jnp.int32),
             pltpu.SMEM((8, 128), jnp.int32),
-            dma((3,)), dma,
+            dma((6,)), dma,
             dma((heads,)), dma((heads, 2)),
             dma, dma((heads,)),
             dma((heads,)), dma((heads, 2, hops)),
@@ -478,7 +489,7 @@
         compiler_params=pltpu.CompilerParams(
             collective_id=0, has_side_effects=True, vmem_limit_bytes=60 * 1024 * 1024),
         name="block_attention",
-    )(*big, selected, counts, block_slot)
+    )(*big)
 
 
 def solution(mesh):

time: 59.3 us -> 58.2 us (0.981)
  Pallas kernels: 57.8 us -> 56.7 us
    pallas_call x1, Pallas kernels: 57.8 us -> 56.7 us  [body(): pl.pallas_call(functools.partial(kernel, ns, nh, heads, entries), out_sha...]
where the time goes in v4:
time: 58.2 us; the launch traced here: 58.1 us
  Pallas kernels  56.7 us (97%)
  local copies, waits for them, and re-layouts  1.32 us (2%)
    pallas_call x1, Pallas kernels, body(): pl.pallas_call(functools.partial(kernel, ns, nh, heads, entries), out_sha...  56.7 us
    unnamed x1, local copies, waits for them, and re-layouts  1.32 us

profile of v4, /device:TPU:0, one launch (start us, length us, event | category | flops | bytes accessed | tf_op | source)
XLA Modules:
  0.0 58.1 jit_solution(76316578638387640)
XLA Ops:
  0.0 56.7 %block_attention.1 = bf16[128,8192]{1,0:T(8,128)(2,1)S(1)} custom-call(bf16[128,8192]{1,0:T(8,128)(2,1)} %q_hbm.1, bf16[128,1024]{1,0:T(8,128)(2,1)} %k_hbm.1, bf16[128,1024]{1,0:T(8,128)(2,1)} %v_hbm.1, s32[4,8]{1,0:T(4,128)} %sel_hbm.1, s32[4]{0:T(128)} %cnt_hbm.1, s32[4]{0:T(128)} %slot_hbm.1), custom_call_target="tpu_custom_call" | custom-call | tf_op jit(solution)/shard_map/block_attention/pallas_call | solution.py:456
  56.7 1.3 %copy.8 = bf16[128,8192]{1,0:T(8,128)(2,1)} copy(bf16[128,8192]{1,0:T(8,128)(2,1)S(1)} %block_attention.1) | data formatting | bytes 4194304

commit v5 on v4

--- a/solution.py
+++ b/solution.py
@@ -20,7 +20,7 @@
 def kernel(ns, nh, heads, entries, q_hbm, k_hbm, v_hbm, sel_hbm, cnt_hbm, slot_hbm, out_ref,
            sel_ref, cnt_ref, own_slot_ref,
            qv, kvin, qbuf, obuf, kcat, vcat, diag, stage, rows_v, rows_s, plan_v, plan_s, place_v, place_s,
-           ins, local_sem, hs, hr, qs, qr, us, ur, ds_, dr, ys, yr, cs, cr, os_, or_, ss, sr, *kv):
+           ins, local_sem, hs, hr, qs, qr, us, ur, ds_, ys, yr, cs, cr, os_, or_, ss, sr, *kv):
     s = lax.axis_index("seq")
     h = lax.axis_index("head")
     ysz = Y_SIZE
@@ -101,20 +101,20 @@
     def head_near(g, role, place):
         return remote(kvin.at[role, :, lanes(side * heads + g, HEAD_SIZE)],
                       kv[g].at[role, z * nh + place],
-                      hs.at[g], hr.at[g, 0], (s, partner))
+                      hs, hr.at[g, 0], (s, partner))
 
     def head_far(g, role):
         return remote(kvin.at[role, :, lanes((1 - side) * heads + g, HEAD_SIZE)],
                       kv[g].at[role, z * nh + h],
-                      hs.at[g], hr.at[g, 1], (s, (1 - side) * half + role))
+                      hs, hr.at[g, 1], (s, (1 - side) * half + role))
 
     def head_far_in(g):
         ref = kv[g].at[c, pl.ds(z * nh + (1 - side) * half, half)]
-        return remote(ref, ref, hs.at[g], hr.at[g, 1], (s, x_peer))
-
-    def head_sent(g):
-        ref = kv[g].at[0, pl.ds(0, nh - 1)]
-        return remote(ref, ref, hs.at[g], hr.at[g, 1], (s, x_peer))
+        return remote(ref, ref, hs, hr.at[g, 1], (s, x_peer))
+
+    def head_sent():
+        ref = kv[0].at[0, pl.ds(0, heads * (nh - 1))]
+        return remote(ref, ref, hs, hr.at[0, 1], (s, x_peer))
 
     def q_head(g):
         return remote(qv.at[:, lanes((1 - side) * heads + g, width)], qbuf.at[g],
@@ -126,11 +126,11 @@
 
     def up(g, p, t, zz, dev):
         ref = part(g, zz, p)
-        return remote(ref, ref, us.at[g], ur.at[g, p, t], (dev, h))
+        return remote(ref, ref, us.at[g], ur.at[g, p, zz], (dev, h))
 
     def down(g, p, t, zz, dev):
         ref = part(g, zz, p)
-        return remote(ref, ref, ds_.at[g], dr.at[g, p, t], (dev, h))
+        return remote(ref, ref, ds_.at[g], ur.at[g, p, zz], (dev, h))
 
     def ups(g, count):
         ref = kv[g].at[c, pl.ds(0, count * nh)]
@@ -138,12 +138,12 @@
 
     def downs(g, count):
         ref = kv[g].at[c, pl.ds((zsz - count) * nh, count * nh)]
-        return remote(ref, ref, ds_.at[g], dr.at[g, 0, 0], (s, h))
+        return remote(ref, ref, ds_.at[g], ur.at[g, 0, 0], (s, h))
 
     def across(g, zz, count):
         return remote(stage.at[g % 2, pl.ds(zz * PER_OWNER, count * PER_OWNER)],
                       kv[g].at[c, pl.ds(zsz * nh + zz * PER_OWNER, count * PER_OWNER)],
-                      ys.at[g], yr.at[g], (y_peer, h))
+                      ys.at[g % 2], yr.at[g], (y_peer, h))
 
     def share(g, start, size, role):
         ref = kv[g].at[role, pl.ds(start, size)]
@@ -224,7 +224,6 @@
         share(g, 0, held, 1 - c).wait_recv()
 
     def drain(g):
-        head_sent(g).wait_send()
         if g + 2 >= heads:
             across(g, 0, zsz).wait_send()
         share(g, 0, held, c).wait_send()
@@ -432,6 +431,7 @@
     for g in range(heads):
         drain(g)
     drain_rows()
+    head_sent().wait_send()
     remote(qbuf, qbuf, qs, qr.at[0], (s, x_peer)).wait_send()
     results().wait_send()
     results().wait_recv()
@@ -477,11 +477,11 @@
             pltpu.VMEM((8, 128), jnp.int32),
             pltpu.SMEM((8, 128), jnp.int32),
             dma((6,)), dma,
-            dma((heads,)), dma((heads, 2)),
+            dma, dma((heads, 2)),
             dma, dma((heads,)),
-            dma((heads,)), dma((heads, 2, hops)),
-            dma((heads,)), dma((heads, 2, hops)),
-            dma((heads,)), dma((heads,)),
+            dma((heads,)), dma((heads, 2, zsz)),
+            dma((heads,)),
+            dma((2,)), dma((heads,)),
             dma((heads,)), dma((heads,)),
             dma, dma,
             dma((1 + 2 * hops,)), dma((1 + 2 * hops,)),

time: 58.2 us -> 58.1 us (level)
  no operation moved by 1% of the time
where the time goes in v5:
time: 58.1 us; the launch traced here: 57.9 us
  Pallas kernels  56.6 us (97%)
  local copies, waits for them, and re-layouts  1.32 us (2%)
    pallas_call x1, Pallas kernels, body(): pl.pallas_call(functools.partial(kernel, ns, nh, heads, entries), out_sha...  56.6 us
    unnamed x1, local copies, waits for them, and re-layouts  1.32 us

profile of v5, /device:TPU:0, one launch (start us, length us, event | category | flops | bytes accessed | tf_op | source)
XLA Modules:
  0.0 57.9 jit_solution(2664852025874459472)
XLA Ops:
  0.0 56.6 %block_attention.1 = bf16[128,8192]{1,0:T(8,128)(2,1)S(1)} custom-call(bf16[128,8192]{1,0:T(8,128)(2,1)} %q_hbm.1, bf16[128,1024]{1,0:T(8,128)(2,1)} %k_hbm.1, bf16[128,1024]{1,0:T(8,128)(2,1)} %v_hbm.1, s32[4,8]{1,0:T(4,128)} %sel_hbm.1, s32[4]{0:T(128)} %cnt_hbm.1, s32[4]{0:T(128)} %slot_hbm.1), custom_call_target="tpu_custom_call" | custom-call | tf_op jit(solution)/shard_map/block_attention/pallas_call | solution.py:456
  56.6 1.3 %copy.8 = bf16[128,8192]{1,0:T(8,128)(2,1)} copy(bf16[128,8192]{1,0:T(8,128)(2,1)S(1)} %block_attention.1) | data formatting | bytes 4194304
